TPU v7x, 256 devices: a whole 4x4x8 slice. The times are simulated.
256 devices in a mesh: row: 16 (over z_lo, y, core), col: 16 (over z_hi, x).
Axes of the slice: x: 4, y: 4, z: 8 (z_hi: 4, z_lo: 2; z = z_hi * 2 + z_lo), core: 2. Of those that a mesh axis runs over, the one named last changes fastest.
Arguments:
- matrix: bfloat16 [6144, 6144], P('row', 'col'), as said below
- polar_factor: bfloat16 [6144, 6144], P('row', 'col'), as said below
- start_basis: bfloat16 [6144, 6144], P('row', 'col'), may hold values from -0.078125 to 0.078125
Outputs:
- gram_halves: float32 [3072, 6144], P('row', 'col')
- projected: float32 [3072, 6144], P('row', 'col')
Inputs may be any that keep to these rules, and one draw needn't show every extreme that they name: `matrix`: symmetric. `polar_factor`: symmetric.
All inputs are finite; a program needn't handle non-finite values.
Results may differ from a plain program's by a relative error of at most 0.017.
Values may be sent and summed in bfloat16 or wider, within the bound.
A program may use at most 64 MiB of HBM per device.

v0:
```python
import jax
import jax.numpy as jnp
from jax import lax
from jax.sharding import PartitionSpec as P


def sent_together(arrays, axis, dim, along):
    both = jnp.concatenate(arrays, axis=along)
    whole, at, finished = (lax.all_gather(both, axis, axis=dim, tiled=True), 0, [])
    for a in arrays:
        finished.append(lax.slice_in_dim(whole, at, at + a.shape[along], axis=along))
        at += a.shape[along]
    return tuple(finished)


def in_blocks(value, dim, length):
    before, after = (value.shape[:dim], value.shape[dim + 1 :])
    return jnp.moveaxis(value.reshape(*before, length, -1, *after), dim, 0)


def sum_at_owner(value, axis, dim):
    length = lax.axis_size(axis)
    blocks = lax.all_to_all(in_blocks(value, dim, length), axis, 0, 0, tiled=True)
    return jnp.sum(blocks.astype(jnp.float32), axis=0)


def transposed_product(left, right):
    return lax.dot_general(
        left, right, (((0,), (0,)), ((), ())), preferred_element_type=jnp.float32
    )


def per_device(matrix, polar_factor, start_basis):
    local_rows, width = start_basis.shape
    col_count = lax.axis_size("col")
    half_block = width // 2
    half_width = half_block * col_count
    sign = jnp.where(jnp.arange(width) < half_block, 1.0, -1.0).astype(jnp.float32)
    start_cols = lax.all_gather(start_basis, "row", axis=0, tiled=True)
    polar_panel, matrix_panel = sent_together((polar_factor, matrix), "col", 1, 0)
    product = jnp.dot(polar_panel, start_cols, preferred_element_type=jnp.float32)
    basis = ((start_basis.astype(jnp.float32) + sign * product) * 0.5).astype(jnp.bfloat16)
    basis_cols = lax.all_gather(basis, "row", axis=0, tiled=True)
    image = jnp.dot(matrix_panel, basis_cols, preferred_element_type=jnp.float32)
    image = image.astype(jnp.bfloat16)
    basis_rows = lax.all_gather(basis, "col", axis=1, tiled=True)
    split_rows = basis_rows.reshape(local_rows, col_count, 2, half_block)
    left_first = split_rows[:, :, 0, :].reshape(local_rows, half_width)
    left_second = split_rows[:, :, 1, :].reshape(local_rows, half_width)
    right_first = jnp.concatenate([basis[:, :half_block], image[:, :half_block]], axis=1)
    right_second = jnp.concatenate([basis[:, half_block:], image[:, half_block:]], axis=1)
    first_terms = transposed_product(left_first, right_first)
    second_terms = transposed_product(left_second, right_second)
    summed = sum_at_owner(
        jnp.concatenate(
            [
                first_terms[:, :half_block],
                second_terms[:, :half_block],
                first_terms[:, half_block:],
                second_terms[:, half_block:],
            ],
            axis=1,
        ).astype(jnp.bfloat16),
        "row",
        0,
    )
    return (summed[:, :width], summed[:, width:])


def solution(mesh):
    return jax.shard_map(
        per_device,
        mesh=mesh,
        in_specs=(P("row", "col"), P("row", "col"), P("row", "col")),
        out_specs=(P("row", "col"), P("row", "col")),
        check_vma=False,
    )
```

profile of v0, /device:TPU:1, one launch (start us, length us, event | category | flops | bytes accessed | tf_op | source)
XLA Modules:
  0.0 414.5 jit_solution(11632365746241983339)
XLA Ops:
  7.2 0.7 all-gather.7.cloned.1.call-update
  7.9 1.9 pad_maximum_fusion.1
  10.0 1.2 copy.6
  11.1 43.4 %all-gather.7.cloned.1.call-done = bf16[6144,384]{1,0:T(8,128)(2,1)} async-done(((bf16[384,384]{1,0:T(8,128)(2,1)}), bf16[6144,384]{1,0:T(8,128)(2,1)}) %all-gather.7.cloned.1.call-update) | async-done | bytes 4718608 | tf_op jit(solution)/shard_map/all_gather | solution.py:39
  54.5 136.8 %all-gather.5.cloned.1.call-done = bf16[768,6144]{1,0:T(8,128)(2,1)} async-done(((bf16[768,384]{1,0:T(8,128)(2,1)}), bf16[768,6144]{1,0:T(8,128)(2,1)}) %all-gather.5.cloned.1.call-update) | async-done | bytes 9437200 | tf_op jit(solution)/shard_map/all_gather | solution.py:9
  191.3 7.1 %fusion.16 = bf16[384,384]{0,1:T(8,128)(2,1)} fusion(bf16[6144,384]{1,0:T(8,128)(2,1)} %all-gather.7.cloned.1.call-done, bf16[768,6144]{1,0:T(8,128)(2,1)} %all-gather.5.cloned.1.call-done, bf16[384,384]{0,1:T(8,128)(2,1)S(1)} %copy.6, f32[384]{0:T(512)S(1)} %fusion.25), kind=kOutput, calls=%fused_computation.12 | convolution fusion | flops 1812676608 | bytes 10028544 | tf_op jit(solution)/shard_map/dot_general | solution.py:41
  199.0 1.7 fusion.32
  200.7 37.6 %all-gather.11.cloned.1.call-done = bf16[6144,384]{0,1:T(8,128)(2,1)} async-done(((bf16[384,384]{0,1:T(8,128)(2,1)}), bf16[6144,384]{0,1:T(8,128)(2,1)}) %all-gather.11.cloned.1.call-update) | async-done | bytes 4718608 | tf_op jit(solution)/shard_map/all_gather | solution.py:43
  238.3 6.4 %fusion.13 = bf16[384,384]{0,1:T(8,128)(2,1)S(1)} fusion(bf16[6144,384]{0,1:T(8,128)(2,1)} %all-gather.11.cloned.1.call-done, bf16[768,6144]{1,0:T(8,128)(2,1)} %all-gather.5.cloned.1.call-done), kind=kOutput, calls=%fused_computation.11 | convolution fusion | flops 1812086784 | bytes 9732096 | tf_op jit(solution)/shard_map/dot_general | solution.py:44
  244.7 0.7 fusion.33
  245.4 73.8 %all-gather.9.cloned.1.call-done = bf16[384,6144]{0,1:T(8,128)(2,1)} async-done(((bf16[384,384]{0,1:T(8,128)(2,1)}), bf16[384,6144]{0,1:T(8,128)(2,1)}) %all-gather.9.cloned.1.call-update) | async-done | bytes 4718608 | tf_op jit(solution)/shard_map/all_gather | solution.py:46
  319.2 2.9 fusion.28
  322.0 1.4 convolution_convert_fusion.1
  323.5 1.2 fusion.29
  324.7 2.5 copy.14
  327.2 1.5 copy.16
  328.7 2.4 convolution_convert_fusion
  331.2 1.6 fusion.30
  332.7 2.7 copy.15
  335.4 2.5 copy.17
  338.0 4.5 %pad_maximum_fusion = bf16[16,192,768]{2,1,0:T(8,128)(2,1)S(1)} fusion(bf16[16,192,192]{2,1,0:T(8,128)(2,1)} %bitcast.16, bf16[16,192,192]{2,1,0:T(8,128)(2,1)S(1)} %bitcast.14, bf16[16,192,192]{2,1,0:T(8,128)(2,1)} %bitcast.15, bf16[16,192,192]{2,1,0:T(8,128)(2,1)S(1)} %bitcast.13), kind=kLoop, calls=%fused_computation.5 | loop fusion | flops 18874368 | bytes 9437184 | tf_op jit(solution)/shard_map/concatenate | solution.py:55
  342.5 63.9 %all_to_all.5 = bf16[16,192,768]{2,1,0:T(8,128)(2,1)S(1)} all-to-all(bf16[16,192,768]{2,1,0:T(8,128)(2,1)S(1)} %pad_maximum_fusion), channel_id=1, replica_groups=mesh['row'=16,'col'=16] {'row'}, dimensions={0} | all-to-all | bytes 9437184 | tf_op jit(solution)/shard_map/all_to_all | solution.py:23
  406.4 0.6 convert_reduce_fusion
  407.1 0.9 fusion.31
  (12 shorter events, 0.7 us)
Async XLA Ops:
  7.2 47.3 %all-gather.7.cloned.1.call-start = ((), (), s32[]{:S(2)}) async-start(), calls=%async_computation.2 | async-start | bytes 5013504 | tf_op jit(solution)/shard_map/all_gather | solution.py:39
  7.9 183.4 %all-gather.5.cloned.1.call-start = ((), (), s32[]{:S(2)}) async-start(), calls=%async_computation.1 | async-start | bytes 10027008 | tf_op jit(solution)/shard_map/all_gather | solution.py:9
  9.9 228.4 %all-gather.11.cloned.1.call-start = ((), (), s32[]{:S(2)}) async-start(), calls=%async_computation.4 | async-start | bytes 5013504 | tf_op jit(solution)/shard_map/all_gather | solution.py:43
  198.4 120.8 %all-gather.9.cloned.1.call-start = ((), (), s32[]{:S(2)}) async-start(), calls=%async_computation.3 | async-start | bytes 5013504 | tf_op jit(solution)/shard_map/all_gather | solution.py:46
  331.1 6.8 %copy-start = (bf16[3072,192]{1,0:T(8,128)(2,1)S(1)}, bf16[3072,192]{1,0:T(8,128)(2,1)}, u32[]{:S(2)}) copy-start(bf16[3072,192]{1,0:T(8,128)(2,1)} %copy.14) | copy-start | bytes 3538948
  331.1 6.8 %copy-start.1 = (bf16[3072,192]{1,0:T(8,128)(2,1)S(1)}, bf16[3072,192]{1,0:T(8,128)(2,1)}, u32[]{:S(2)}) copy-start(bf16[3072,192]{1,0:T(8,128)(2,1)} %copy.16) | copy-start | bytes 3538948
Sparse Core Ops, SparseCore 0:
  9.8 44.6 all-gather.6
  56.9 134.3 all-gather.4
  198.5 39.7 all-gather.10
  241.2 77.9 all-gather.8
where the time goes:
time: 415 us; the launch traced here: 414 us
  waiting for transfers between devices  293 us (71%)
  blocking collectives  63.9 us (15%)
  local copies, waits for them, and re-layouts  19.3 us (5%)
  matrix products  17.4 us (4%)
  between operations  13.8 us (3%)
  other arithmetic  7.08 us (2%)
    all_gather x1, waiting for transfers between devices, sent_together(): lax.all_gather(both, axis, axis=dim, tiled=True)  137 us
    all_gather x1, waiting for transfers between devices, per_device(): basis_rows = lax.all_gather(basis, 'col', axis=1, tiled=True)  73.8 us
    all_to_all x1, blocking collectives, sum_at_owner(): lax.all_to_all(in_blocks(value, dim, length), axis, 0, 0, tiled=True)  63.9 us
    all_gather x1, waiting for transfers between devices, per_device(): start_cols = lax.all_gather(start_basis, 'row', axis=0, tiled=True)  43.4 us
    all_gather x1, waiting for transfers between devices, per_device(): basis_cols = lax.all_gather(basis, 'row', axis=0, tiled=True)  37.6 us
    concatenate x4, local copies, waits for them, and re-layouts, per_device(): jnp.concatenate([first_terms[:, :half_block], second_terms[:, :half_block...  9.32 us
  transfers between devices with their start and end apart: 4, of which 4 were waited for; matrix products, arithmetic and copies ran while one was open for 3% of the time, Pallas kernels for 0%

commit v1 on v0

v1 whole, which is shorter than its diff:
```python
import jax
import jax.numpy as jnp
from jax import lax
from jax.experimental import pallas as pl
from jax.experimental.pallas import tpu as pltpu
from jax.sharding import PartitionSpec as P

BF16 = jnp.bfloat16
F32 = jnp.float32
SIDES = (-1, 1)
N_SEMS = 178
X_ROWS = 64


def kernel(
    p_in, m_in, s_in, gram_out, proj_out,
    p_panel, m_panel, t_panel, s_panel, b_panel, i_panel,
    turned, total, total2, send_sems, recv_sems,
):
    width = s_in.shape[0]
    half = width // 2
    row, col = lax.axis_index("row"), lax.axis_index("col")
    core, y, zl = row % 2, (row // 2) % 4, row // 8
    x, zh = col % 4, col // 4

    def device(x=x, y=y, zh=zh, zl=zl, core=core):
        return ((zl * 4 + y) * 2 + core, zh * 4 + x)

    def near(axis, step):
        if axis == "x":
            return device(x=(x + step + 4) % 4)
        if axis == "z":
            return device(zh=(zh + step + 4) % 4)
        return device(y=(y + step + 4) % 4)

    peer = device(zl=1 - zl)
    sibling = device(core=1 - core)
    mirror = (col, row)
    sends = []
    slots = {}

    def slot(key):
        return slots.setdefault(key, len(slots))

    def copy(src, dst, to, key):
        return pltpu.make_async_remote_copy(
            src_ref=src, dst_ref=dst,
            send_sem=send_sems.at[slot(key)], recv_sem=recv_sems.at[slot(key)],
            device_id=to, device_id_type=pl.DeviceIdType.MESH,
        )

    def send(src, dst, to, key):
        one = copy(src, dst, to, key)
        one.start()
        sends.append(one)

    def arrive(ref, key):
        copy(ref, ref, sibling, key).wait_recv()

    class Panel:
        def __init__(self, name, panel, own, at, n, first, second):
            self.name, self.panel, self.own = name, panel, own
            self.whole = pl.ds(at, n)
            self.lower, self.upper = pl.ds(at, n // 2), pl.ds(at + n // 2, n // 2)
            self.first, self.second = first, second

        def part(self, df, ds, rows):
            dz, dx = (df, ds) if self.first == "z" else (ds, df)
            return self.panel.at[((zh + dz + 4) % 4) * 4 + (x + dx + 4) % 4, rows]

        def source(self, df, ds, rows):
            return self.own.at[rows] if df == 0 and ds == 0 else self.part(df, ds, rows)

        def out(self, df, ds, rows, axis, step, *key):
            send(self.source(df, ds, rows), self.part(df, ds, rows), near(axis, step), (self.name,) + key)

        def wait(self, df, ds, rows, *key):
            arrive(self.part(df, ds, rows), (self.name,) + key)

        def f1(self):
            for side in SIDES:
                self.out(0, 0, self.whole, self.first, -side, "f", side)

        def f2(self):
            for side in SIDES:
                self.wait(side, 0, self.whole, "f", side)
                rows = self.lower if side == -1 else self.upper
                self.out(side, 0, rows, self.first, -side, "ff", side)

        def f3(self):
            for side in SIDES:
                self.wait(2, 0, self.lower if side == -1 else self.upper, "ff", side)

        def s1(self, d):
            for side in SIDES:
                self.out(d, 0, self.whole, self.second, -side, "s", d, side)

        def s2(self, d):
            for side in SIDES:
                self.wait(d, side, self.whole, "s", d, side)
                rows = self.lower if side == -1 else self.upper
                self.out(d, side, rows, self.second, -side, "ss", d, side)

        def s3(self, d):
            for side in SIDES:
                self.wait(d, 2, self.lower if side == -1 else self.upper, "ss", d, side)

    class Column:
        def __init__(self, name, panel, own):
            self.name, self.panel, self.own = name, panel, own
            self.whole = pl.ds(0, width)
            self.lower, self.upper = pl.ds(0, half), pl.ds(half, half)

        def part(self, dz, dy, rows, of=core):
            at_z = zl if dz == 0 else 1 - zl
            return self.panel.at[(at_z * 4 + (y + dy + 4) % 4) * 2 + of, rows]

        def out(self, dz, dy, rows, to, *key):
            own = dz == 0 and dy == 0
            src = self.own.at[rows] if own else self.part(dz, dy, rows)
            send(src, self.part(dz, dy, rows), to, (self.name,) + key)

        def wait(self, dz, dy, rows, *key):
            arrive(self.part(dz, dy, rows), (self.name,) + key)

        def r1(self):
            for side in SIDES:
                self.out(0, 0, self.whole, near("y", -side), "y", 0, side)
            self.out(0, 0, self.whole, peer, "z")
            self.out(0, 0, self.whole, sibling, "d", 0, 0)

        def rz(self):
            self.wait(1, 0, self.whole, "z")
            for side in SIDES:
                self.out(1, 0, self.whole, near("y", -side), "y", 1, side)
            self.out(1, 0, self.whole, sibling, "d", 1, 0)

        def r2(self, q):
            for side in SIDES:
                self.wait(q, side, self.whole, "y", q, side)
                rows = self.lower if side == -1 else self.upper
                self.out(q, side, rows, near("y", -side), "yy", q, side)
                self.out(q, side, self.whole, sibling, "d", q, side)

        def r3(self, q):
            for side in SIDES:
                rows = self.lower if side == -1 else self.upper
                self.wait(q, 2, rows, "yy", q, side)
                self.out(q, 2, rows, sibling, "dd", q, side)

        def r4(self):
            other = 1 - core
            for q in (0, 1):
                for dy in (0,) + SIDES:
                    arrive(self.part(q, dy, self.whole, other), (self.name, "d", q, dy))
                for side in SIDES:
                    rows = self.lower if side == -1 else self.upper
                    arrive(self.part(q, 2, rows, other), (self.name, "dd", q, side))

    def two_ways(name, panel, own):
        split = width - X_ROWS
        return (
            Panel(name + "a", panel, own, 0, split, "z", "x"),
            Panel(name + "b", panel, own, split, X_ROWS, "x", "z"),
        )

    def begin(ways):
        a, b = ways
        a.f1()
        b.f1()
        a.s1(0)

    def add_group(dz, left, rights):
        base = ((zh + dz + 4) % 4) * 4

        @pl.loop(0, 4)
        def _(j):
            for right, into in rights:
                into[...] += jnp.dot(left[base + j], right[base + j], preferred_element_type=F32)

    def phase(ways, column, left, rights, then):
        a, b = ways
        b.f2()
        a.s2(0)
        column.r2(0)
        b.f3()
        a.f2()
        a.s1(-1)
        a.s1(1)
        for d in (0, -1, 1, 2):
            b.s1(d)
        column.r3(0)
        a.s2(-1)
        column.rz()
        a.s2(1)
        a.f3()
        a.s1(2)
        column.r2(1)
        for d in (0, -1, 1):
            b.s2(d)
        column.r3(1)
        a.s2(2)
        b.s2(2)
        then()
        a.s3(0)
        column.r4()
        add_group(0, left, rights)
        a.s3(-1)
        add_group(-1, left, rights)
        a.s3(1)
        add_group(1, left, rights)
        a.s3(2)
        for d in (0, -1, 1, 2):
            b.s3(d)
        add_group(2, left, rights)

    barrier = pltpu.get_barrier_semaphore()
    partners = [near(axis, step) for axis in "xyz" for step in SIDES] + [peer, sibling]
    for partner in partners:
        pl.semaphore_signal(barrier, inc=1, device_id=partner, device_id_type=pl.DeviceIdType.MESH)

    @pl.when(row != col)
    def _():
        pl.semaphore_signal(barrier, inc=1, device_id=mirror, device_id_type=pl.DeviceIdType.MESH)
        pl.semaphore_wait(barrier, len(partners) + 1)

    @pl.when(row == col)
    def _():
        pl.semaphore_wait(barrier, len(partners))

    polar = two_ways("p", p_panel, p_in)
    matrix = two_ways("m", m_panel, m_in)
    turned_rows = two_ways("t", t_panel, t_panel.at[col])
    start = Column("s", s_panel, s_in)
    basis = Column("b", b_panel, b_panel.at[row])
    image = Column("i", i_panel, i_panel.at[row])

    begin(polar)
    start.r1()
    p_panel[col] = p_in[...]
    m_panel[col] = m_in[...]
    s_panel[row] = s_in[...]
    total[...] = jnp.zeros_like(total)
    phase(polar, start, p_panel, ((s_panel, total),), lambda: begin(matrix))

    first = lax.broadcasted_iota(jnp.int32, (width, width), 1) < half
    product = total[...]
    value = ((s_in[...].astype(F32) + jnp.where(first, product, -product)) * 0.5).astype(BF16)
    b_panel[row] = value
    turned[...] = jnp.transpose(value.astype(F32)).astype(BF16)
    total[...] = jnp.zeros_like(total)
    basis.r1()
    to_mirror = copy(turned, t_panel.at[row], mirror, "turn")

    @pl.when(row != col)
    def _():
        to_mirror.start()

    @pl.when(row == col)
    def _():
        t_panel[col] = turned[...]

    def begin_turned():
        @pl.when(row != col)
        def _():
            copy(t_panel.at[col], t_panel.at[col], mirror, "turn").wait_recv()

        begin(turned_rows)

    phase(matrix, basis, m_panel, ((b_panel, total),), begin_turned)

    i_panel[row] = total[...].astype(BF16)
    total[...] = jnp.zeros_like(total)
    total2[...] = jnp.zeros_like(total2)
    image.r1()
    phase(turned_rows, image, t_panel, ((b_panel, total), (i_panel, total2)), lambda: None)

    keep = lax.broadcasted_iota(jnp.int32, (half, width), 1) < half
    gram_out[...] = jnp.where(keep, total[:half], total[half:])
    proj_out[...] = jnp.where(keep, total2[:half], total2[half:])

    for one in sends:
        one.wait_send()

    @pl.when(row != col)
    def _():
        to_mirror.wait_send()


def per_device(matrix, polar_factor, start_basis):
    width = start_basis.shape[0]
    blocks = 16
    vmem = pl.BlockSpec(memory_space=pltpu.VMEM)
    out = jax.ShapeDtypeStruct((width // 2, width), F32)
    panel = pltpu.VMEM((blocks, width, width), BF16)
    return pl.pallas_call(
        kernel,
        out_shape=(out, out),
        in_specs=[vmem] * 3,
        out_specs=(vmem, vmem),
        scratch_shapes=[panel] * 6
        + [
            pltpu.VMEM((width, width), BF16),
            pltpu.VMEM((width, width), F32),
            pltpu.VMEM((width, width), F32),
            pltpu.SemaphoreType.DMA((N_SEMS,)),
            pltpu.SemaphoreType.DMA((N_SEMS,)),
        ],
        compiler_params=pltpu.CompilerParams(
            collective_id=0, has_side_effects=True, vmem_limit_bytes=48 * 1024 * 1024
        ),
    )(polar_factor, matrix, start_basis)


def solution(mesh):
    return jax.shard_map(
        per_device,
        mesh=mesh,
        in_specs=(P("row", "col"), P("row", "col"), P("row", "col")),
        out_specs=(P("row", "col"), P("row", "col")),
        check_vma=False,
    )
```

time: 415 us -> 155 us (0.37)
  waiting for transfers between devices: 293 us -> 0 us
  Pallas kernels: 0 us -> 150 us
  blocking collectives: 63.9 us -> 0 us
  matrix products: 17.4 us -> 0 us
  local copies, waits for them, and re-layouts: 19.3 us -> 4.31 us
  between operations: 13.8 us -> 0.65 us
  other arithmetic: 7.08 us -> 0 us
    all_gather x4 -> x0, waiting for transfers between devices: 292 us -> none  [the longest x1 137 us: sent_together(): lax.all_gather(both, axis, axis=dim, tiled=True)]
    pallas_call x0 -> x1, Pallas kernels: none -> 150 us  [per_device(): pl.pallas_call(kernel, out_shape=(out, out), in_specs=[vmem] * 3, out_spe...]
    all_to_all x1 -> x0, blocking collectives: 63.9 us -> none  [sum_at_owner(): lax.all_to_all(in_blocks(value, dim, length), axis, 0, 0, tiled=True)]
    dot_general x4 -> x0, matrix products: 17.4 us -> none  [the longest x1 7.14 us: per_device(): jnp.dot(polar_panel, start_cols, preferred_element_type=jnp.float32)]
    concatenate x4 -> x0, local copies, waits for them, and re-layouts: 9.32 us -> none  [per_device(): jnp.concatenate([first_terms[:, :half_block], second_terms[:, :half_block...]
    slice x6 -> x0, local copies, waits for them, and re-layouts: 8.8 us -> none  [the longest x1 2.85 us: per_device(): left_first = split_rows[:, :, 0, :].reshape(local_rows, half_width)]
    concatenate x2 -> x0, other arithmetic: 6.43 us -> none  [the longest x1 4.48 us: per_device(): jnp.concatenate([first_terms[:, :half_block], second_terms[:, :half_block...]
  transfers between devices with their start and end apart: 4 -> 0, of which waited for: 4 -> 0; matrix products, arithmetic and copies ran while one was open for 3% -> 0% of each run, Pallas kernels for 0% -> 0%
where the time goes in v1:
time: 155 us
  Pallas kernels  150 us (97%)
  local copies, waits for them, and re-layouts  4.31 us (3%)
    pallas_call x1, Pallas kernels, per_device(): pl.pallas_call(kernel, out_shape=(out, out), in_specs=[vmem] * 3, out_spe...  150 us
    unnamed x8, local copies, waits for them, and re-layouts  4.31 us

profile of v1, /device:TPU:1, one launch (start us, length us, event | category | flops | bytes accessed | tf_op | source)
XLA Modules:
  0.0 155.1 jit_solution(4813583723148148067)
XLA Ops:
  0.6 0.0 copy-start
  0.6 1.0 copy-done
  1.6 0.0 copy-start.1
  1.6 1.0 copy-done.1
  2.6 0.0 copy-start.2
  2.6 1.0 copy-done.2
  3.5 150.1 %shard_map.50 = (f32[192,384]{1,0:T(8,128)S(1)}, f32[192,384]{1,0:T(8,128)S(1)}) custom-call(bf16[384,384]{1,0:T(8,128)(2,1)S(1)} %copy-done, bf16[384,384]{1,0:T(8,128)(2,1)S(1)} %copy-done.1, bf16[384,384]{1,0:T(8,128)(2,1)S(1)} %copy-done.2), custom_call_target="tpu_custom_call" | custom-call | tf_op jit(solution)/shard_map/pallas_call | solution.py:296
  153.7 0.7 copy.7
  154.4 0.7 copy.8
Async XLA Ops:
  0.6 1.0 copy-start
  1.6 1.0 copy-start.1
  2.6 1.0 copy-start.2

commit v2 on v1

v2 whole, which is shorter than its diff:
```python
import jax
import jax.numpy as jnp
from jax import lax
from jax.experimental import pallas as pl
from jax.experimental.pallas import tpu as pltpu
from jax.sharding import PartitionSpec as P

BF16 = jnp.bfloat16
F32 = jnp.float32
SIDES = (-1, 1)
N_SEMS = 118
X_ROWS = (64, 64, 64)


def kernel(
    p_in, m_in, s_in, gram_out, proj_out,
    p_panel, m_panel, t_panel, s_panel, b_panel, i_panel,
    turned, total, total2, send_sems, recv_sems,
):
    width, blocks = total.shape[0], p_panel.shape[0]
    half = width // 2
    row, col = lax.axis_index("row"), lax.axis_index("col")
    core, y, zl = row % 2, (row // 2) % 4, row // 8
    x, zh = col % 4, col // 4

    def device(x=x, y=y, zh=zh, zl=zl, core=core):
        return ((zl * 4 + y) * 2 + core, zh * 4 + x)

    def near(axis, step):
        if axis == "x":
            return device(x=(x + step + 4) % 4)
        if axis == "z":
            return device(zh=(zh + step + 4) % 4)
        return device(y=(y + step + 4) % 4)

    peer = device(zl=1 - zl)
    sibling = device(core=1 - core)
    mirror = (col, row)
    slots = {}

    def slot(key):
        return slots.setdefault(key, len(slots))

    def copy(src, dst, to, key):
        return pltpu.make_async_remote_copy(
            src_ref=src, dst_ref=dst,
            send_sem=send_sems.at["psmbtiu".index(key[0][0])], recv_sem=recv_sems.at[slot(key)],
            device_id=to, device_id_type=pl.DeviceIdType.MESH,
        )

    def send(src, dst, to, key):
        copy(src, dst, to, key).start()

    def arrive(ref, key):
        copy(ref, ref, sibling, key).wait_recv()

    def pairs(ds):
        return [(d, side) for d in ds or (0, -1, 1, 2) for side in SIDES]

    inputs = {"pa": p_in, "pb": p_in, "ma": m_in, "mb": m_in, "s": s_in}

    class Panel:
        def __init__(self, name, panel, at, n, first, second):
            self.name, self.panel = name, panel
            self.whole = pl.ds(at, n)
            self.lower, self.upper = pl.ds(at, n // 2), pl.ds(at + n // 2, n // 2)
            self.first, self.second = first, second

        def part(self, df, ds, rows):
            dz, dx = (df, ds) if self.first == "z" else (ds, df)
            return self.panel.at[((zh + dz + 4) % 4) * 4 + (x + dx + 4) % 4, rows]

        def out(self, df, ds, rows, axis, step, *key):
            src = self.part(df, ds, rows)
            if df == 0 and ds == 0 and self.name in inputs:
                src = inputs[self.name].at[rows]
            send(src, self.part(df, ds, rows), near(axis, step), (self.name,) + key)

        def wait(self, df, ds, rows, *key):
            arrive(self.part(df, ds, rows), (self.name,) + key)

        def f1(self):
            for side in SIDES:
                self.out(0, 0, self.whole, self.first, -side, "f", side)

        def f2(self):
            for side in SIDES:
                self.wait(side, 0, self.whole, "f", side)
                rows = self.lower if side == -1 else self.upper
                self.out(side, 0, rows, self.first, -side, "ff")

        def f3(self):
            self.wait(2, 0, self.whole, "ff")

        def s1(self, *ds):
            for d, side in pairs(ds):
                self.out(d, 0, self.whole, self.second, -side, "s", d, side)

        def s2(self, *ds):
            for d, side in pairs(ds):
                self.wait(d, side, self.whole, "s", d, side)
                rows = self.lower if side == -1 else self.upper
                self.out(d, side, rows, self.second, -side, "ss", d)

        def s3(self, *ds):
            for d in ds or (0, -1, 1, 2):
                self.wait(d, 2, self.whole, "ss", d)

    class Column:
        def __init__(self, name, panel):
            self.name, self.panel = name, panel
            self.whole = pl.ds(0, width)
            self.lower, self.upper = pl.ds(0, half), pl.ds(half, half)

        def part(self, dz, dy, rows, of=core):
            at_z = zl if dz == 0 else 1 - zl
            return self.panel.at[(at_z * 4 + (y + dy + 4) % 4) * 2 + of, rows]

        def out(self, dz, dy, rows, to, *key):
            src = self.part(dz, dy, rows)
            if dz == 0 and dy == 0 and self.name in inputs:
                src = inputs[self.name].at[rows]
            send(src, self.part(dz, dy, rows), to, (self.name,) + key)

        def wait(self, dz, dy, rows, *key):
            arrive(self.part(dz, dy, rows), (self.name,) + key)

        def r1(self):
            for side in SIDES:
                self.out(0, 0, self.whole, near("y", -side), "y", 0, side)
            self.out(0, 0, self.whole, peer, "z")
            self.out(0, 0, self.whole, sibling, "d", 0)

        def rz(self):
            self.wait(1, 0, self.whole, "z")
            for side in SIDES:
                self.out(1, 0, self.whole, near("y", -side), "y", 1, side)
            self.out(1, 0, self.whole, sibling, "d", 1)

        def r2(self, q):
            for side in SIDES:
                self.wait(q, side, self.whole, "y", q, side)
                rows = self.lower if side == -1 else self.upper
                self.out(q, side, rows, near("y", -side), "yy", q)
                self.out(q, side, self.whole, sibling, "d", q)

        def r3(self, q):
            self.wait(q, 2, self.whole, "yy", q)
            self.out(q, 2, self.whole, sibling, "d", q)

        def r4(self, *qs):
            for q in qs or (0, 1):
                arrive(self.panel.at[pl.ds(0, 4)], (self.name, "d", q))

    def two_ways(name, panel, rows):
        split = width - rows
        return (
            Panel(name + "a", panel, 0, split, "z", "x"),
            Panel(name + "b", panel, split, rows, "x", "z"),
        )

    def add_group(dz, left, right, into):
        base = ((zh + dz + 4) % 4) * 4

        @pl.loop(0, 4)
        def _(j):
            into[...] += jnp.dot(left[base + j], right[base + j], preferred_element_type=F32)

    barrier = pltpu.get_barrier_semaphore()
    partners = [near(axis, step) for axis in "xyz" for step in SIDES] + [peer, sibling]
    for partner in partners:
        pl.semaphore_signal(barrier, inc=1, device_id=partner, device_id_type=pl.DeviceIdType.MESH)

    @pl.when(row != col)
    def _():
        pl.semaphore_signal(barrier, inc=1, device_id=mirror, device_id_type=pl.DeviceIdType.MESH)
        pl.semaphore_wait(barrier, len(partners) + 1)

    @pl.when(row == col)
    def _():
        pl.semaphore_wait(barrier, len(partners))

    pa, pb = two_ways("p", p_panel, X_ROWS[0])
    ma, mb = two_ways("m", m_panel, X_ROWS[1])
    ta, tb = two_ways("t", t_panel, X_ROWS[2])
    start = Column("s", s_panel)
    basis = Column("b", b_panel)
    image = Column("i", i_panel)
    to_mirror = copy(turned, t_panel.at[row], mirror, ("u",))

    pa.f1()
    pb.f1()
    pa.s1(0)
    start.r1()
    p_panel[col] = p_in[...]
    s_panel[row] = s_in[...]
    m_panel[col] = m_in[...]
    total[...] = jnp.zeros_like(total)
    pb.f2()
    pa.s2(0)
    start.r2(0)
    pb.f3()
    pa.f2()
    pa.s1(-1)
    pa.s1(1)
    pa.s2(-1)
    start.rz()
    pb.s1()
    pa.s2(1)
    pa.f3()
    pa.s1(2)
    pb.s2(0)
    start.r2(1)
    pb.s2(-1, 1, 2)
    ma.f1()
    pa.s2(2)
    mb.f1()
    ma.s1(0)
    start.r3(0)
    start.r3(1)
    start.r4()
    for d in (0, -1, 1):
        pa.s3(d)
        add_group(d, p_panel, s_panel, total)
    pa.s3(2)
    pb.s3()
    add_group(2, p_panel, s_panel, total)

    first = lax.broadcasted_iota(jnp.int32, (width, width), 1) < half
    product = total[...]
    value = ((s_panel[row].astype(F32) + jnp.where(first, product, -product)) * 0.5).astype(BF16)
    b_panel[row] = value
    turned[...] = jnp.transpose(value.astype(F32)).astype(BF16)
    total[...] = jnp.zeros_like(total)
    basis.r1()

    @pl.when(row != col)
    def _():
        to_mirror.start()

    @pl.when(row == col)
    def _():
        t_panel[col] = turned[...]

    mb.f2()
    ma.s2(0)
    ma.f2()
    ma.s1(-1)
    ma.s1(1)
    mb.f3()
    basis.r2(0)
    basis.rz()
    mb.s1()
    ma.s2(-1)
    ma.s2(1)
    ma.f3()
    ma.s1(2)
    mb.s2(0)
    basis.r2(1)
    mb.s2(-1, 1, 2)

    @pl.when(row != col)
    def _():
        copy(t_panel.at[col], t_panel.at[col], mirror, ("u",)).wait_recv()

    ta.f1()
    ma.s2(2)
    tb.f1()
    ta.s1(0)
    basis.r3(0)
    basis.r3(1)
    basis.r4()
    for d in (0, -1, 1):
        ma.s3(d)
        add_group(d, m_panel, b_panel, total)
    ma.s3(2)
    mb.s3()
    add_group(2, m_panel, b_panel, total)
    i_panel[row] = total[...].astype(BF16)
    total[...] = jnp.zeros_like(total)
    total2[...] = jnp.zeros_like(total2)
    image.r1()
    tb.f2()
    ta.s2(0)
    ta.f2()
    ta.s1(-1)
    ta.s1(1)
    tb.f3()
    image.r2(0)
    image.rz()
    tb.s1()
    ta.s2(-1)
    ta.s2(1)
    ta.f3()
    ta.s1(2)
    tb.s2(0)
    image.r2(1)
    tb.s2(-1, 1, 2)
    ta.s2(2)
    image.r3(0)
    for d in (0, -1, 1):
        ta.s3(d)
        add_group(d, t_panel, b_panel, total)
    image.r3(1)
    image.r4()
    for d in (0, -1, 1):
        add_group(d, t_panel, i_panel, total2)
    ta.s3(2)
    tb.s3()
    add_group(2, t_panel, b_panel, total)
    add_group(2, t_panel, i_panel, total2)

    assert len(slots) == N_SEMS
    keep = lax.broadcasted_iota(jnp.int32, (half, width), 1) < half
    gram_out[...] = jnp.where(keep, total[:half], total[half:])
    proj_out[...] = jnp.where(keep, total2[:half], total2[half:])

    for panel, name in ((p_panel, "p"), (s_panel, "s"), (m_panel, "m"), (b_panel, "b"), (t_panel, "t"), (i_panel, "i")):
        sent = panel.at[pl.ds(0, blocks - 1)]
        copy(sent, sent, sibling, (name + "a", "f", 1) if name in "pmt" else (name, "z")).wait_send()

    @pl.when(row != col)
    def _():
        to_mirror.wait_send()


def per_device(matrix, polar_factor, start_basis):
    width = start_basis.shape[0]
    blocks = 16
    vmem = pl.BlockSpec(memory_space=pltpu.VMEM)
    out = jax.ShapeDtypeStruct((width // 2, width), F32)
    panel = pltpu.VMEM((blocks, width, width), BF16)
    return pl.pallas_call(
        kernel,
        out_shape=(out, out),
        in_specs=[vmem] * 3,
        out_specs=(vmem, vmem),
        scratch_shapes=[panel] * 6
        + [
            pltpu.VMEM((width, width), BF16),
            pltpu.VMEM((width, width), F32),
            pltpu.VMEM((width, width), F32),
            pltpu.SemaphoreType.DMA((7,)),
            pltpu.SemaphoreType.DMA((N_SEMS,)),
        ],
        compiler_params=pltpu.CompilerParams(
            collective_id=0, has_side_effects=True, vmem_limit_bytes=48 * 1024 * 1024
        ),
    )(polar_factor, matrix, start_basis)


def solution(mesh):
    return jax.shard_map(
        per_device,
        mesh=mesh,
        in_specs=(P("row", "col"), P("row", "col"), P("row", "col")),
        out_specs=(P("row", "col"), P("row", "col")),
        check_vma=False,
    )
```

time: 155 us -> 149 us (0.961)
  Pallas kernels: 150 us -> 143 us
    pallas_call x1, Pallas kernels: 150 us -> 143 us  [per_device(): pl.pallas_call(kernel, out_shape=(out, out), in_specs=[vmem] * 3, out_spe...]
where the time goes in v2:
time: 149 us; the launch traced here: 148 us
  Pallas kernels  143 us (96%)
  local copies, waits for them, and re-layouts  4.31 us (3%)
    pallas_call x1, Pallas kernels, per_device(): pl.pallas_call(kernel, out_shape=(out, out), in_specs=[vmem] * 3, out_spe...  143 us
    unnamed x8, local copies, waits for them, and re-layouts  4.31 us

profile of v2, /device:TPU:1, one launch (start us, length us, event | category | flops | bytes accessed | tf_op | source)
XLA Modules:
  0.0 148.4 jit_solution(17018056387502582946)
XLA Ops:
  0.6 0.0 copy-start
  0.6 1.0 copy-done
  1.6 0.0 copy-start.1
  1.6 1.0 copy-done.1
  2.6 0.0 copy-start.2
  2.6 1.0 copy-done.2
  3.5 143.5 %shard_map.50 = (f32[192,384]{1,0:T(8,128)S(1)}, f32[192,384]{1,0:T(8,128)S(1)}) custom-call(bf16[384,384]{1,0:T(8,128)(2,1)S(1)} %copy-done, bf16[384,384]{1,0:T(8,128)(2,1)S(1)} %copy-done.1, bf16[384,384]{1,0:T(8,128)(2,1)S(1)} %copy-done.2), custom_call_target="tpu_custom_call" | custom-call | tf_op jit(solution)/shard_map/pallas_call | solution.py:333
  147.0 0.7 copy.7
  147.7 0.7 copy.8
Async XLA Ops:
  0.6 1.0 copy-start
  1.6 1.0 copy-start.1
  2.6 1.0 copy-start.2

commit v3 on v2

--- a/solution.py
+++ b/solution.py
@@ -209,6 +209,7 @@
     pa.s2(1)
     pa.f3()
     pa.s1(2)
+    start.r3(0)
     pb.s2(0)
     start.r2(1)
     pb.s2(-1, 1, 2)
@@ -216,9 +217,9 @@
     pa.s2(2)
     mb.f1()
     ma.s1(0)
-    start.r3(0)
     start.r3(1)
-    start.r4()
+    start.r4(0)
+    start.r4(1)
     for d in (0, -1, 1):
         pa.s3(d)
         add_group(d, p_panel, s_panel, total)
@@ -255,6 +256,7 @@
     ma.s2(1)
     ma.f3()
     ma.s1(2)
+    basis.r3(0)
     mb.s2(0)
     basis.r2(1)
     mb.s2(-1, 1, 2)
@@ -264,12 +266,12 @@
         copy(t_panel.at[col], t_panel.at[col], mirror, ("u",)).wait_recv()
 
     ta.f1()
+    basis.r3(1)
     ma.s2(2)
     tb.f1()
     ta.s1(0)
-    basis.r3(0)
-    basis.r3(1)
-    basis.r4()
+    basis.r4(0)
+    basis.r4(1)
     for d in (0, -1, 1):
         ma.s3(d)
         add_group(d, m_panel, b_panel, total)
@@ -290,18 +292,19 @@
     image.rz()
     tb.s1()
     ta.s2(-1)
+    ta.s3(0)
+    add_group(0, t_panel, b_panel, total)
     ta.s2(1)
     ta.f3()
     ta.s1(2)
-    tb.s2(0)
+    image.r3(0)
     image.r2(1)
-    tb.s2(-1, 1, 2)
-    ta.s2(2)
-    image.r3(0)
-    for d in (0, -1, 1):
+    tb.s2()
+    for d in (-1, 1):
         ta.s3(d)
         add_group(d, t_panel, b_panel, total)
     image.r3(1)
+    ta.s2(2)
     image.r4()
     for d in (0, -1, 1):
         add_group(d, t_panel, i_panel, total2)

time: 149 us -> 144 us (0.966); the launches traced: 148 us -> 141 us
  Pallas kernels: 143 us -> 136 us
    pallas_call x1, Pallas kernels: 143 us -> 136 us  [per_device(): pl.pallas_call(kernel, out_shape=(out, out), in_specs=[vmem] * 3, out_spe...]
where the time goes in v3:
time: 144 us; the launch traced here: 141 us
  Pallas kernels  136 us (94%)
  local copies, waits for them, and re-layouts  4.31 us (3%)
    pallas_call x1, Pallas kernels, per_device(): pl.pallas_call(kernel, out_shape=(out, out), in_specs=[vmem] * 3, out_spe...  136 us
    unnamed x8, local copies, waits for them, and re-layouts  4.31 us

profile of v3, /device:TPU:1, one launch (start us, length us, event | category | flops | bytes accessed | tf_op | source)
XLA Modules:
  0.0 141.2 jit_solution(2202319998767076792)
XLA Ops:
  0.6 0.0 copy-start
  0.6 1.0 copy-done
  1.6 0.0 copy-start.1
  1.6 1.0 copy-done.1
  2.6 0.0 copy-start.2
  2.6 1.0 copy-done.2
  3.5 136.2 %shard_map.50 = (f32[192,384]{1,0:T(8,128)S(1)}, f32[192,384]{1,0:T(8,128)S(1)}) custom-call(bf16[384,384]{1,0:T(8,128)(2,1)S(1)} %copy-done, bf16[384,384]{1,0:T(8,128)(2,1)S(1)} %copy-done.1, bf16[384,384]{1,0:T(8,128)(2,1)S(1)} %copy-done.2), custom_call_target="tpu_custom_call" | custom-call | tf_op jit(solution)/shard_map/pallas_call | solution.py:336
  139.8 0.7 copy.7
  140.5 0.7 copy.8
Async XLA Ops:
  0.6 1.0 copy-start
  1.6 1.0 copy-start.1
  2.6 1.0 copy-start.2
